TPU v7x, 256 devices: a whole 4x4x8 slice. The times are simulated.
256 devices in a mesh: grp: 8 (over z), sp: 32 (over y, x, core).
Axes of the slice: x: 4, y: 4, z: 8, core: 2. Of those that a mesh axis runs over, the one named last changes fastest.
Arguments:
- tokens: bfloat16 [16384, 2880], P(('grp', 'sp')), may hold values from -36 to 36
- query_weight: bfloat16 [2880, 2048], P(None, 'sp'), may hold values from -0.109375 to 0.109375
- key_value_weight: bfloat16 [2880, 1024], replicated, may hold values from -0.109375 to 0.109375
- block_places: int32 [32], replicated, may hold values from 0 to 31, each once
- sinks: float32 [32], replicated, may hold values from -1 to 5
Outputs:
- attended: bfloat16 [16384, 2048], P(('grp', 'sp'))
Inputs may be any that keep to these rules, and one draw needn't show every extreme that they name: `block_places`: every sequence block appears once.
All inputs are finite; a program needn't handle non-finite values.
Results may differ from a plain program's by a relative error of at most 0.008.
The roundings to bfloat16 on the way count: a program that leaves them out, or rounds other values in their place, can miss the bound.
Values may be sent and summed in bfloat16 or wider, within the bound.
A program may use at most 128 MiB of HBM per device.

v0:
```python
import jax
import jax.numpy as jnp
from jax import lax
from jax.sharding import PartitionSpec as P

QUERY_HEADS = 32
HEAD_SIZE = 64
BPG = 4
rope_base = 150000.0
neg_large = -1e30


def joined_along(pieces, dim):
    pieces = jnp.moveaxis(pieces, 0, dim)
    shape = pieces.shape
    return pieces.reshape(*shape[:dim], shape[dim] * shape[dim + 1], *shape[dim + 2 :])


def piecewise(value, axis, dim, apply, out_dim):
    size, span = (lax.axis_size(axis), value.shape[dim])
    count = 2 if span % 2 == 0 else 1
    finished, length = ([], span // count)
    for k in range(count):
        share = lax.slice_in_dim(value, k * length, (k + 1) * length, axis=dim)
        starts = jnp.arange(size) * span + k * length
        finished.append(jax.vmap(apply)(lax.all_gather(share, axis), starts))
    return joined_along(jnp.concatenate(finished, axis=out_dim + 1), out_dim)


def rotate(vectors, angles):
    middle = vectors.shape[-1] // 2
    first_half = vectors[..., :middle]
    second_half = vectors[..., middle:]
    cosine = jnp.cos(angles)
    sine_part = jnp.sin(angles)
    return jnp.concatenate(
        [
            first_half * cosine - second_half * sine_part,
            second_half * cosine + first_half * sine_part,
        ],
        axis=-1,
    )


def locate(stored, block_rows, block_places):
    blocks = stored // block_rows
    table = jnp.arange(block_places.shape[0], dtype=jnp.int32)
    onehot = (blocks[:, None] == table[None, :]).astype(jnp.int32)
    return jnp.sum(onehot * block_places[None, :], axis=1) * block_rows + stored % block_rows


def prepare(projected, own_places, query_cols, kv_cols, head_count):
    row_count = projected.shape[0]
    inverse = rope_base ** (-(jnp.arange(HEAD_SIZE // 2, dtype=jnp.float32) * 2.0) / HEAD_SIZE)
    angles = own_places.astype(jnp.float32)[:, None, None] * inverse[None, None, :]
    queries = rotate(
        projected[:, :query_cols].reshape(row_count, query_cols // HEAD_SIZE, HEAD_SIZE), angles
    ).astype(jnp.bfloat16)
    rotated_keys = rotate(
        projected[:, query_cols : query_cols + kv_cols].reshape(row_count, head_count, HEAD_SIZE),
        angles,
    )
    key_value_pair = jnp.concatenate(
        [rotated_keys.reshape(row_count, kv_cols), projected[:, query_cols + kv_cols :]], axis=1
    ).astype(jnp.bfloat16)
    return (queries, key_value_pair)


def attend(state, queries, query_places, key_value_pair, key_places, head_count):
    maxima, totals, mixture = state
    key_count = key_value_pair.shape[0]
    column_half = key_value_pair.shape[1] // 2
    key_part = key_value_pair[:, :column_half].reshape(key_count, head_count, HEAD_SIZE)
    value_part = key_value_pair[:, column_half:].reshape(key_count, head_count, HEAD_SIZE)
    scores = jnp.einsum(
        "qhgd,khd->hgqk", queries, key_part, preferred_element_type=jnp.float32
    ) * HEAD_SIZE ** (-0.5)
    allowed = key_places[None, :] <= query_places[:, None]
    scores = jnp.where(allowed, scores, neg_large)
    updated = jnp.maximum(maxima, jnp.max(scores, axis=-1))
    weights = jnp.where(allowed, jnp.exp(scores - updated[..., None]), 0.0)
    factor = jnp.exp(maxima - updated)
    totals = totals * factor + jnp.sum(weights, axis=-1)
    mixture = mixture * factor[..., None] + jnp.einsum(
        "hgqk,khd->hgqd",
        weights.astype(jnp.bfloat16),
        value_part,
        preferred_element_type=jnp.float32,
    )
    return (updated, totals, mixture)


def per_device(tokens, query_weight, key_value_weight, block_places, sinks):
    sp_count = lax.axis_size("sp")
    local_rows = tokens.shape[0]
    group_rows = local_rows * sp_count
    block_rows = group_rows // BPG
    kv_total = key_value_weight.shape[1] // (2 * HEAD_SIZE)
    sp_place = lax.axis_index("sp")
    grp_place = lax.axis_index("grp")
    query_cols = query_weight.shape[1]
    query_heads = query_cols // HEAD_SIZE
    head_count = max(kv_total // sp_count, 1)
    kv_cols = head_count * HEAD_SIZE
    first_head = sp_place * query_heads // (QUERY_HEADS // kv_total)
    key_weight = lax.dynamic_slice_in_dim(key_value_weight, first_head * HEAD_SIZE, kv_cols, 1)
    value_weight = lax.dynamic_slice_in_dim(
        key_value_weight, kv_total * HEAD_SIZE + first_head * HEAD_SIZE, kv_cols, 1
    )
    joined = jnp.concatenate([query_weight, key_weight, value_weight], axis=1)

    def project(piece, start):
        return jnp.dot(piece, joined, preferred_element_type=jnp.float32)

    projected = piecewise(tokens, "sp", 0, project, 0)
    query_local = jnp.arange(group_rows, dtype=jnp.int32)
    head_first = sp_place * query_heads
    own_places = locate(grp_place * group_rows + query_local, block_rows, block_places)
    queries, key_value_pair = prepare(projected, own_places, query_cols, kv_cols, head_count)
    query_sharing = query_heads // head_count
    head_sinks = lax.dynamic_slice_in_dim(sinks, head_first, query_heads, 0).reshape(
        head_count, query_sharing
    )
    sink_rows = jnp.broadcast_to(head_sinks[:, :, None], (head_count, query_sharing, group_rows))
    query_block4 = queries.reshape(group_rows, head_count, query_sharing, HEAD_SIZE)
    initial = (
        sink_rows,
        jnp.ones((head_count, query_sharing, group_rows), jnp.float32),
        jnp.zeros((head_count, query_sharing, group_rows, HEAD_SIZE), jnp.float32),
    )
    piece = lax.all_gather(key_value_pair, "grp", axis=0, tiled=True)
    step_rows = min(piece.shape[0], group_rows)
    turns = piece.shape[0] // step_rows

    def visit(turn, inner):
        offset = turn * step_rows
        piece_rows = lax.dynamic_slice_in_dim(piece, offset, step_rows, 0)
        position = offset + jnp.arange(step_rows, dtype=jnp.int32)
        stored = position // group_rows * group_rows + position % group_rows
        key_places = locate(stored, block_rows, block_places)
        return attend(inner, query_block4, own_places, piece_rows, key_places, head_count)

    maxima, totals, mixture = lax.fori_loop(0, turns, visit, initial)
    normed = jnp.transpose(mixture, (2, 0, 1, 3)) / jnp.transpose(totals, (2, 0, 1))[..., None]
    attended = normed.reshape(group_rows, query_cols).astype(jnp.bfloat16)
    return lax.all_to_all(attended, "sp", split_axis=0, concat_axis=1, tiled=True)


def solution(mesh):
    in_specs = (P(("grp", "sp"), None), P(None, "sp"), P(), P(), P())
    out_specs = P(("grp", "sp"), None)
    return jax.shard_map(
        per_device, mesh=mesh, in_specs=in_specs, out_specs=out_specs, check_vma=False
    )
```

profile of v0, /device:TPU:1, one launch (start us, length us, event | category | flops | bytes accessed | tf_op | source)
XLA Modules:
  0.0 353.2 jit_solution(3869679549317436455)
XLA Ops:
  11.8 55.8 %all-gather.8.cloned.1.call-done = bf16[1024,2880]{1,0:T(8,128)(2,1)} async-done(((bf16[32,2880]{1,0:T(8,128)(2,1)}), bf16[1024,2880]{1,0:T(8,128)(2,1)}) %all-gather.8.cloned.1.call-update) | async-done | bytes 5898256 | tf_op jit(solution)/shard_map/all_gather | solution.py:26
  67.6 4.5 %convolution_bitcast_fusion.1 = f32[32,32,192]{2,1,0:T(8,128)S(1)} fusion(bf16[32,32,2880]{2,1,0:T(8,128)(2,1)} %bitcast.94, bf16[2880,64]{0,1:T(8,128)(2,1)S(1)} %copy.44, bf16[2880,64]{0,1:T(8,128)(2,1)S(1)} %copy.43, bf16[2880,64]{0,1:T(8,128)(2,1)S(1)} %copy-done.2), kind=kOutput, calls=%fused_computation.49 | convolution fusion | flops 1135779840 | bytes 7790592 | tf_op jit(solution)/shard_map/vmap()/dot_general | solution.py:113
  72.1 50.5 %all-gather.10.cloned.1.call-done = bf16[1024,2880]{1,0:T(8,128)(2,1)} async-done(((bf16[32,2880]{1,0:T(8,128)(2,1)}), bf16[1024,2880]{1,0:T(8,128)(2,1)}) %all-gather.10.cloned.1.call-update) | async-done | bytes 5898256 | tf_op jit(solution)/shard_map/all_gather | solution.py:26
  122.6 4.5 %convolution_bitcast_fusion = f32[32,32,192]{2,1,0:T(8,128)S(1)} fusion(bf16[32,32,2880]{2,1,0:T(8,128)(2,1)} %bitcast.95, bf16[2880,64]{0,1:T(8,128)(2,1)S(1)} %copy.44, bf16[2880,64]{0,1:T(8,128)(2,1)S(1)} %copy.43, bf16[2880,64]{0,1:T(8,128)(2,1)S(1)} %copy-done.2), kind=kOutput, calls=%fused_computation.48 | convolution fusion | flops 1135779840 | bytes 7790592 | tf_op jit(solution)/shard_map/vmap()/dot_general | solution.py:113
  131.3 52.6 %all-gather.6.cloned.1.call-done = bf16[16384,128]{0,1:T(8,128)(2,1)} async-done(((bf16[2048,128]{0,1:T(8,128)(2,1)}), bf16[16384,128]{0,1:T(8,128)(2,1)}) %all-gather.6.cloned.1.call-update) | async-done | bytes 4194320 | tf_op jit(solution)/shard_map/all_gather | solution.py:131
  184.5 141.5 %while.21 = (s32[]{:T(128)}, f32[1,1,2048]{2,1,0:T(1,128)S(1)}, f32[1,1,2048]{2,1,0:T(1,128)S(1)}, f32[1,1,2048,64]{2,3,1,0:T(8,128)S(1)}, s32[32]{0:T(128)S(1)}...) while((s32[]{:T(128)}, f32[1,1,2048]{2,1,0:T(1,128)S(1)}, ...), condition=%wide.region_5.6_spmd.clone, body=%wide.region_1.5_spmd.clone.sunk | while | flops 1141592064 | bytes 119497064 | solution.py:143
  188.3 5.3 %fusion.75 = f32[2048]{0:T(1024)S(1)} fusion(f32[2048,2048]{1,0:T(8,128)S(1)} %get-tuple-element.393, f32[2048]{0:T(1024)S(1)} %bitcast.86, s32[2048]{0:T(1024)S(1)} %get-tuple-element.427, s32[2048]{0:T(1024)S(1)} %fusion.73), kind=kLoop, calls=%fused_computation.4.clone.1 | loop fusion | flops 25163776 | bytes 16809984 | tf_op jit(solution)/shard_map/while/body/eval_jaxpr/reduce_sum | solution.py:83
  194.1 8.1 %fusion.77 = f32[1,1,2048,64]{2,3,1,0:T(8,128)S(1)} fusion(f32[2048,2048]{1,0:T(8,128)} %copy-done, f32[2048]{0:T(1024)S(1)} %bitcast.87, s32[2048]{0:T(1024)S(1)} %get-tuple-element.427, s32[2048]{0:T(1024)S(1)} %fusion.73, f32[1,1,2048,64]{2,3,1,0:T(8,128)S(1)} %get-tuple-element.412, bf16[16384,128]{0,1:T(8,128)(2,1)} %get-tuple-element.428, ...), kind=kOutput, calls=%fused_computation.8.clone.1 | convolution fusion | flops 562429952 | bytes 18120712 | tf_op jit(solution)/shard_map/while/body/eval_jaxpr/hgqk,khd->hgqd/dot_general | solution.py:84
  202.4 3.6 %fusion.74 = (f32[2048]{0:T(1024)S(1)}, f32[2048,2048]{1,0:T(8,128)S(1)}) fusion(s32[2048]{0:T(1024)S(1)} %get-tuple-element.427, s32[2048]{0:T(1024)S(1)} %fusion.73, bf16[2048,1,1,64]{0,3,2,1:T(8,128)(2,1)S(1)} %get-tuple-element.429, bf16[16384,128]{0,1:T(8,128)(2,1)} %get-tuple-element.428, s32[]{:T(128)S(6)} %select_n.248), kind=kOutput, calls=%fused_computation.2.clone.1 | convolution fusion | flops 553646080 | bytes 17326084 | tf_op jit(solution)/shard_map/while/body/eval_jaxpr/qhgd,khd->hgqk/dot_general | solution.py:75
  206.0 5.3 %fusion.75 = f32[2048]{0:T(1024)S(1)} fusion(f32[2048,2048]{1,0:T(8,128)S(1)} %get-tuple-element.393, f32[2048]{0:T(1024)S(1)} %bitcast.86, s32[2048]{0:T(1024)S(1)} %get-tuple-element.427, s32[2048]{0:T(1024)S(1)} %fusion.73), kind=kLoop, calls=%fused_computation.4.clone.1 | loop fusion | flops 25163776 | bytes 16809984 | tf_op jit(solution)/shard_map/while/body/eval_jaxpr/reduce_sum | solution.py:83
  211.8 8.1 %fusion.77 = f32[1,1,2048,64]{2,3,1,0:T(8,128)S(1)} fusion(f32[2048,2048]{1,0:T(8,128)} %copy-done, f32[2048]{0:T(1024)S(1)} %bitcast.87, s32[2048]{0:T(1024)S(1)} %get-tuple-element.427, s32[2048]{0:T(1024)S(1)} %fusion.73, f32[1,1,2048,64]{2,3,1,0:T(8,128)S(1)} %get-tuple-element.412, bf16[16384,128]{0,1:T(8,128)(2,1)} %get-tuple-element.428, ...), kind=kOutput, calls=%fused_computation.8.clone.1 | convolution fusion | flops 562429952 | bytes 18120712 | tf_op jit(solution)/shard_map/while/body/eval_jaxpr/hgqk,khd->hgqd/dot_general | solution.py:84
  223.7 5.3 %fusion.75 = f32[2048]{0:T(1024)S(1)} fusion(f32[2048,2048]{1,0:T(8,128)S(1)} %get-tuple-element.393, f32[2048]{0:T(1024)S(1)} %bitcast.86, s32[2048]{0:T(1024)S(1)} %get-tuple-element.427, s32[2048]{0:T(1024)S(1)} %fusion.73), kind=kLoop, calls=%fused_computation.4.clone.1 | loop fusion | flops 25163776 | bytes 16809984 | tf_op jit(solution)/shard_map/while/body/eval_jaxpr/reduce_sum | solution.py:83
  229.5 8.1 %fusion.77 = f32[1,1,2048,64]{2,3,1,0:T(8,128)S(1)} fusion(f32[2048,2048]{1,0:T(8,128)} %copy-done, f32[2048]{0:T(1024)S(1)} %bitcast.87, s32[2048]{0:T(1024)S(1)} %get-tuple-element.427, s32[2048]{0:T(1024)S(1)} %fusion.73, f32[1,1,2048,64]{2,3,1,0:T(8,128)S(1)} %get-tuple-element.412, bf16[16384,128]{0,1:T(8,128)(2,1)} %get-tuple-element.428, ...), kind=kOutput, calls=%fused_computation.8.clone.1 | convolution fusion | flops 562429952 | bytes 18120712 | tf_op jit(solution)/shard_map/while/body/eval_jaxpr/hgqk,khd->hgqd/dot_general | solution.py:84
  241.4 5.3 %fusion.75 = f32[2048]{0:T(1024)S(1)} fusion(f32[2048,2048]{1,0:T(8,128)S(1)} %get-tuple-element.393, f32[2048]{0:T(1024)S(1)} %bitcast.86, s32[2048]{0:T(1024)S(1)} %get-tuple-element.427, s32[2048]{0:T(1024)S(1)} %fusion.73), kind=kLoop, calls=%fused_computation.4.clone.1 | loop fusion | flops 25163776 | bytes 16809984 | tf_op jit(solution)/shard_map/while/body/eval_jaxpr/reduce_sum | solution.py:83
  247.1 8.1 %fusion.77 = f32[1,1,2048,64]{2,3,1,0:T(8,128)S(1)} fusion(f32[2048,2048]{1,0:T(8,128)} %copy-done, f32[2048]{0:T(1024)S(1)} %bitcast.87, s32[2048]{0:T(1024)S(1)} %get-tuple-element.427, s32[2048]{0:T(1024)S(1)} %fusion.73, f32[1,1,2048,64]{2,3,1,0:T(8,128)S(1)} %get-tuple-element.412, bf16[16384,128]{0,1:T(8,128)(2,1)} %get-tuple-element.428, ...), kind=kOutput, calls=%fused_computation.8.clone.1 | convolution fusion | flops 562429952 | bytes 18120712 | tf_op jit(solution)/shard_map/while/body/eval_jaxpr/hgqk,khd->hgqd/dot_general | solution.py:84
  259.1 5.3 %fusion.75 = f32[2048]{0:T(1024)S(1)} fusion(f32[2048,2048]{1,0:T(8,128)S(1)} %get-tuple-element.393, f32[2048]{0:T(1024)S(1)} %bitcast.86, s32[2048]{0:T(1024)S(1)} %get-tuple-element.427, s32[2048]{0:T(1024)S(1)} %fusion.73), kind=kLoop, calls=%fused_computation.4.clone.1 | loop fusion | flops 25163776 | bytes 16809984 | tf_op jit(solution)/shard_map/while/body/eval_jaxpr/reduce_sum | solution.py:83
  264.8 8.1 %fusion.77 = f32[1,1,2048,64]{2,3,1,0:T(8,128)S(1)} fusion(f32[2048,2048]{1,0:T(8,128)} %copy-done, f32[2048]{0:T(1024)S(1)} %bitcast.87, s32[2048]{0:T(1024)S(1)} %get-tuple-element.427, s32[2048]{0:T(1024)S(1)} %fusion.73, f32[1,1,2048,64]{2,3,1,0:T(8,128)S(1)} %get-tuple-element.412, bf16[16384,128]{0,1:T(8,128)(2,1)} %get-tuple-element.428, ...), kind=kOutput, calls=%fused_computation.8.clone.1 | convolution fusion | flops 562429952 | bytes 18120712 | tf_op jit(solution)/shard_map/while/body/eval_jaxpr/hgqk,khd->hgqd/dot_general | solution.py:84
  276.8 5.3 %fusion.75 = f32[2048]{0:T(1024)S(1)} fusion(f32[2048,2048]{1,0:T(8,128)S(1)} %get-tuple-element.393, f32[2048]{0:T(1024)S(1)} %bitcast.86, s32[2048]{0:T(1024)S(1)} %get-tuple-element.427, s32[2048]{0:T(1024)S(1)} %fusion.73), kind=kLoop, calls=%fused_computation.4.clone.1 | loop fusion | flops 25163776 | bytes 16809984 | tf_op jit(solution)/shard_map/while/body/eval_jaxpr/reduce_sum | solution.py:83
  282.5 8.1 %fusion.77 = f32[1,1,2048,64]{2,3,1,0:T(8,128)S(1)} fusion(f32[2048,2048]{1,0:T(8,128)} %copy-done, f32[2048]{0:T(1024)S(1)} %bitcast.87, s32[2048]{0:T(1024)S(1)} %get-tuple-element.427, s32[2048]{0:T(1024)S(1)} %fusion.73, f32[1,1,2048,64]{2,3,1,0:T(8,128)S(1)} %get-tuple-element.412, bf16[16384,128]{0,1:T(8,128)(2,1)} %get-tuple-element.428, ...), kind=kOutput, calls=%fused_computation.8.clone.1 | convolution fusion | flops 562429952 | bytes 18120712 | tf_op jit(solution)/shard_map/while/body/eval_jaxpr/hgqk,khd->hgqd/dot_general | solution.py:84
  294.5 5.3 %fusion.75 = f32[2048]{0:T(1024)S(1)} fusion(f32[2048,2048]{1,0:T(8,128)S(1)} %get-tuple-element.393, f32[2048]{0:T(1024)S(1)} %bitcast.86, s32[2048]{0:T(1024)S(1)} %get-tuple-element.427, s32[2048]{0:T(1024)S(1)} %fusion.73), kind=kLoop, calls=%fused_computation.4.clone.1 | loop fusion | flops 25163776 | bytes 16809984 | tf_op jit(solution)/shard_map/while/body/eval_jaxpr/reduce_sum | solution.py:83
  300.2 8.1 %fusion.77 = f32[1,1,2048,64]{2,3,1,0:T(8,128)S(1)} fusion(f32[2048,2048]{1,0:T(8,128)} %copy-done, f32[2048]{0:T(1024)S(1)} %bitcast.87, s32[2048]{0:T(1024)S(1)} %get-tuple-element.427, s32[2048]{0:T(1024)S(1)} %fusion.73, f32[1,1,2048,64]{2,3,1,0:T(8,128)S(1)} %get-tuple-element.412, bf16[16384,128]{0,1:T(8,128)(2,1)} %get-tuple-element.428, ...), kind=kOutput, calls=%fused_computation.8.clone.1 | convolution fusion | flops 562429952 | bytes 18120712 | tf_op jit(solution)/shard_map/while/body/eval_jaxpr/hgqk,khd->hgqd/dot_general | solution.py:84
  312.2 5.3 %fusion.75 = f32[2048]{0:T(1024)S(1)} fusion(f32[2048,2048]{1,0:T(8,128)S(1)} %get-tuple-element.393, f32[2048]{0:T(1024)S(1)} %bitcast.86, s32[2048]{0:T(1024)S(1)} %get-tuple-element.427, s32[2048]{0:T(1024)S(1)} %fusion.73), kind=kLoop, calls=%fused_computation.4.clone.1 | loop fusion | flops 25163776 | bytes 16809984 | tf_op jit(solution)/shard_map/while/body/eval_jaxpr/reduce_sum | solution.py:83
  317.9 8.1 %fusion.77 = f32[1,1,2048,64]{2,3,1,0:T(8,128)S(1)} fusion(f32[2048,2048]{1,0:T(8,128)} %copy-done, f32[2048]{0:T(1024)S(1)} %bitcast.87, s32[2048]{0:T(1024)S(1)} %get-tuple-element.427, s32[2048]{0:T(1024)S(1)} %fusion.73, f32[1,1,2048,64]{2,3,1,0:T(8,128)S(1)} %get-tuple-element.412, bf16[16384,128]{0,1:T(8,128)(2,1)} %get-tuple-element.428, ...), kind=kOutput, calls=%fused_computation.8.clone.1 | convolution fusion | flops 562429952 | bytes 18120712 | tf_op jit(solution)/shard_map/while/body/eval_jaxpr/hgqk,khd->hgqd/dot_general | solution.py:84
  328.4 16.4 %all_to_all.16 = bf16[32,2,2048]{2,1,0:T(2,128)(2,1)S(1)} all-to-all(bf16[32,2,2048]{2,1,0:T(2,128)(2,1)S(1)} %reshape.437), channel_id=1, replica_groups=mesh['grp'=8,'sp'=32] {'sp'}, dimensions={0} | all-to-all | bytes 524288 | tf_op jit(solution)/shard_map/all_to_all | solution.py:146
  (114 shorter events, 43.9 us)
Async XLA Ops:
  6.5 5.1 %copy-start.1 = (s32[32]{0:T(128)S(1)}, s32[32]{0:T(128)}, u32[]{:S(2)}) copy-start(s32[32]{0:T(128)} %param.10) | copy-start | bytes 388
  6.5 61.1 %copy-start.2 = (bf16[2880,64]{0,1:T(8,128)(2,1)S(1)}, bf16[2880,64]{0,1:T(8,128)(2,1)}, u32[]{:S(2)}) copy-start(bf16[2880,64]{0,1:T(8,128)(2,1)} %param.8) | copy-start | bytes 1105924
  6.5 61.1 %all-gather.8.cloned.1.call-start = ((), (), s32[]{:S(2)}) async-start(), calls=%async_computation.2 | async-start | bytes 6217728 | tf_op jit(solution)/shard_map/all_gather | solution.py:26
  8.4 114.2 %all-gather.10.cloned.1.call-start = ((), (), s32[]{:S(2)}) async-start(), calls=%async_computation.3 | async-start | bytes 6217728 | tf_op jit(solution)/shard_map/all_gather | solution.py:26
  9.1 174.8 %all-gather.6.cloned.1.call-start = ((), (), s32[]{:S(2)}) async-start(), calls=%async_computation.1 | async-start | bytes 4718592 | tf_op jit(solution)/shard_map/all_gather | solution.py:131
  127.3 3.4 copy-start.3
  188.3 5.7 %copy-start = (f32[2048,2048]{1,0:T(8,128)}, f32[2048,2048]{1,0:T(8,128)S(1)}, u32[]{:S(2)}) copy-start(f32[2048,2048]{1,0:T(8,128)S(1)} %get-tuple-element.393) | copy-start | bytes 50331652 | tf_op jit(solution)/shard_map/while
  206.0 5.7 %copy-start = (f32[2048,2048]{1,0:T(8,128)}, f32[2048,2048]{1,0:T(8,128)S(1)}, u32[]{:S(2)}) copy-start(f32[2048,2048]{1,0:T(8,128)S(1)} %get-tuple-element.393) | copy-start | bytes 50331652 | tf_op jit(solution)/shard_map/while
  223.7 5.7 %copy-start = (f32[2048,2048]{1,0:T(8,128)}, f32[2048,2048]{1,0:T(8,128)S(1)}, u32[]{:S(2)}) copy-start(f32[2048,2048]{1,0:T(8,128)S(1)} %get-tuple-element.393) | copy-start | bytes 50331652 | tf_op jit(solution)/shard_map/while
  241.4 5.7 %copy-start = (f32[2048,2048]{1,0:T(8,128)}, f32[2048,2048]{1,0:T(8,128)S(1)}, u32[]{:S(2)}) copy-start(f32[2048,2048]{1,0:T(8,128)S(1)} %get-tuple-element.393) | copy-start | bytes 50331652 | tf_op jit(solution)/shard_map/while
  259.1 5.7 %copy-start = (f32[2048,2048]{1,0:T(8,128)}, f32[2048,2048]{1,0:T(8,128)S(1)}, u32[]{:S(2)}) copy-start(f32[2048,2048]{1,0:T(8,128)S(1)} %get-tuple-element.393) | copy-start | bytes 50331652 | tf_op jit(solution)/shard_map/while
  276.8 5.7 %copy-start = (f32[2048,2048]{1,0:T(8,128)}, f32[2048,2048]{1,0:T(8,128)S(1)}, u32[]{:S(2)}) copy-start(f32[2048,2048]{1,0:T(8,128)S(1)} %get-tuple-element.393) | copy-start | bytes 50331652 | tf_op jit(solution)/shard_map/while
  294.5 5.7 %copy-start = (f32[2048,2048]{1,0:T(8,128)}, f32[2048,2048]{1,0:T(8,128)S(1)}, u32[]{:S(2)}) copy-start(f32[2048,2048]{1,0:T(8,128)S(1)} %get-tuple-element.393) | copy-start | bytes 50331652 | tf_op jit(solution)/shard_map/while
  312.2 5.7 %copy-start = (f32[2048,2048]{1,0:T(8,128)}, f32[2048,2048]{1,0:T(8,128)S(1)}, u32[]{:S(2)}) copy-start(f32[2048,2048]{1,0:T(8,128)S(1)} %get-tuple-element.393) | copy-start | bytes 50331652 | tf_op jit(solution)/shard_map/while
Sparse Core Ops, SparseCore 0:
  9.9 57.7 all-gather.7
  70.2 52.4 all-gather.9
  130.8 53.0 all-gather.5
where the time goes:
time: 354 us; the launch traced here: 353 us
  waiting for transfers between devices  160 us (45%)
  matrix products  103 us (29%)
  other arithmetic  47.6 us (13%)
  blocking collectives  16.4 us (5%)
  between operations  13.3 us (4%)
  local copies, waits for them, and re-layouts  12.9 us (4%)
    all_gather x2, waiting for transfers between devices, piecewise(): finished.append(jax.vmap(apply)(lax.all_gather(share, axis), starts))  106 us
    dot_general x8, matrix products, attend(): jnp.einsum('hgqk,khd->hgqd', weights.astype(jnp.bfloat16), value_part, pr...  65 us
    all_gather x1, waiting for transfers between devices, per_device(): piece = lax.all_gather(key_value_pair, 'grp', axis=0, tiled=True)  52.6 us
    reduce_sum x8, other arithmetic, attend(): totals = totals * factor + jnp.sum(weights, axis=-1)  42.5 us
    dot_general x8, matrix products, attend(): jnp.einsum('qhgd,khd->hgqk', queries, key_part, preferred_element_type=jn...  28.7 us
    all_to_all x1, blocking collectives, per_device(): lax.all_to_all(attended, 'sp', split_axis=0, concat_axis=1, tiled=True)  16.4 us
    dot_general x2, matrix products, project(): return jnp.dot(piece, joined, preferred_element_type=jnp.float32)  9.01 us
  transfers between devices with their start and end apart: 3, of which 3 were waited for; matrix products, arithmetic and copies ran while one was open for 2% of the time, Pallas kernels for 0%

commit v1 on v0

--- a/solution.py
+++ b/solution.py
@@ -8,6 +8,12 @@
 BPG = 4
 rope_base = 150000.0
 neg_large = -1e30
+
+
+def replace_the_domain(x_part):
+    return jnp.concatenate(
+        lax.all_to_all(jnp.stack([x_part for _ in range(lax.axis_size("grp"))], 0), "grp", 0, 0), 0
+    )
 
 
 def joined_along(pieces, dim):
@@ -128,7 +134,7 @@
         jnp.ones((head_count, query_sharing, group_rows), jnp.float32),
         jnp.zeros((head_count, query_sharing, group_rows, HEAD_SIZE), jnp.float32),
     )
-    piece = lax.all_gather(key_value_pair, "grp", axis=0, tiled=True)
+    piece = replace_the_domain(key_value_pair)
     step_rows = min(piece.shape[0], group_rows)
     turns = piece.shape[0] // step_rows
 

time: 354 us -> 408 us (1.15)
  waiting for transfers between devices: 160 us -> 203 us
  starting transfers between devices: 0.08 us -> 6.78 us
    all_to_all x0 -> x1, waiting for transfers between devices: none -> 96.2 us  [replace_the_domain(): lax.all_to_all(jnp.stack([x_part for _ in range(lax.axis_size('grp'))], 0...]
    all_gather x1 -> x0, waiting for transfers between devices: 52.6 us -> none  [per_device(): piece = lax.all_gather(key_value_pair, 'grp', axis=0, tiled=True)]
    all_to_all x0 -> x1, starting transfers between devices: none -> 6.74 us  [replace_the_domain(): lax.all_to_all(jnp.stack([x_part for _ in range(lax.axis_size('grp'))], 0...]
    dot_general x8, matrix products: 28.7 us -> 32.8 us  [attend(): jnp.einsum('qhgd,khd->hgqk', queries, key_part, preferred_element_type=jn...]
where the time goes in v1:
time: 408 us
  waiting for transfers between devices  203 us (50%)
  matrix products  107 us (26%)
  other arithmetic  46.8 us (11%)
  local copies, waits for them, and re-layouts  15.6 us (4%)
  blocking collectives  13.6 us (3%)
  between operations  13.6 us (3%)
  starting transfers between devices  6.78 us (2%)
    all_gather x2, waiting for transfers between devices, piecewise(): finished.append(jax.vmap(apply)(lax.all_gather(share, axis), starts))  106 us
    all_to_all x1, waiting for transfers between devices, replace_the_domain(): lax.all_to_all(jnp.stack([x_part for _ in range(lax.axis_size('grp'))], 0...  96.2 us
    dot_general x8, matrix products, attend(): jnp.einsum('hgqk,khd->hgqd', weights.astype(jnp.bfloat16), value_part, pr...  65.4 us
    reduce_sum x8, other arithmetic, attend(): totals = totals * factor + jnp.sum(weights, axis=-1)  42.5 us
    dot_general x8, matrix products, attend(): jnp.einsum('qhgd,khd->hgqk', queries, key_part, preferred_element_type=jn...  32.8 us
    all_to_all x1, blocking collectives, per_device(): lax.all_to_all(attended, 'sp', split_axis=0, concat_axis=1, tiled=True)  13.6 us
    dot_general x2, matrix products, project(): return jnp.dot(piece, joined, preferred_element_type=jnp.float32)  9.01 us
  transfers between devices with their start and end apart: 3, of which 3 were waited for; matrix products, arithmetic and copies ran while one was open for 2% of the time, Pallas kernels for 0%

profile of v1, /device:TPU:1, one launch (start us, length us, event | category | flops | bytes accessed | tf_op | source)
XLA Modules:
  0.0 407.5 jit_solution(3602182995603889070)
XLA Ops:
  11.8 55.8 %all-gather.5.cloned.1.call-done = bf16[1024,2880]{1,0:T(8,128)(2,1)} async-done(((bf16[32,2880]{1,0:T(8,128)(2,1)}), bf16[1024,2880]{1,0:T(8,128)(2,1)}) %all-gather.5.cloned.1.call-update) | async-done | bytes 5898256 | tf_op jit(solution)/shard_map/all_gather | solution.py:32
  67.6 4.5 %convolution_bitcast_fusion.1 = f32[32,32,192]{2,1,0:T(8,128)S(1)} fusion(bf16[32,32,2880]{2,1,0:T(8,128)(2,1)} %bitcast.95, bf16[2880,64]{0,1:T(8,128)(2,1)S(1)} %copy.43, bf16[2880,64]{0,1:T(8,128)(2,1)S(1)} %copy.42, bf16[2880,64]{0,1:T(8,128)(2,1)S(1)} %copy-done.2), kind=kOutput, calls=%fused_computation.49 | convolution fusion | flops 1135779840 | bytes 7790592 | tf_op jit(solution)/shard_map/vmap()/dot_general | solution.py:119
  72.1 50.5 %all-gather.7.cloned.1.call-done = bf16[1024,2880]{1,0:T(8,128)(2,1)} async-done(((bf16[32,2880]{1,0:T(8,128)(2,1)}), bf16[1024,2880]{1,0:T(8,128)(2,1)}) %all-gather.7.cloned.1.call-update) | async-done | bytes 5898256 | tf_op jit(solution)/shard_map/all_gather | solution.py:32
  122.6 4.5 %convolution_bitcast_fusion = f32[32,32,192]{2,1,0:T(8,128)S(1)} fusion(bf16[32,32,2880]{2,1,0:T(8,128)(2,1)} %bitcast.96, bf16[2880,64]{0,1:T(8,128)(2,1)S(1)} %copy.43, bf16[2880,64]{0,1:T(8,128)(2,1)S(1)} %copy.42, bf16[2880,64]{0,1:T(8,128)(2,1)S(1)} %copy-done.2), kind=kOutput, calls=%fused_computation.48 | convolution fusion | flops 1135779840 | bytes 7790592 | tf_op jit(solution)/shard_map/vmap()/dot_general | solution.py:119
  132.7 6.7 %all-to-all-start = ((bf16[8,2048,128]{2,1,0:T(8,128)(2,1)}), bf16[8,2048,128]{2,1,0:T(8,128)(2,1)}, u32[]{:S(2)}, u32[]{:S(2)}) async-start(bf16[8,2048,128]{2,1,0:T(8,128)(2,1)} %stack.2), calls=%async_computation | async-start | bytes 8388608 | tf_op jit(solution)/shard_map/all_to_all | solution.py:15
  140.0 96.2 %all-to-all-done = bf16[8,2048,128]{2,1,0:T(8,128)(2,1)} async-done(((bf16[8,2048,128]{2,1,0:T(8,128)(2,1)}), bf16[8,2048,128]{2,1,0:T(8,128)(2,1)}, u32[]{:S(2)}, u32[]{:S(2)}) %all-to-all-start) | async-done | bytes 4194336 | tf_op jit(solution)/shard_map/all_to_all | solution.py:15
  236.9 146.0 %while.21 = (s32[]{:T(128)}, f32[1,1,2048]{2,1,0:T(1,128)S(1)}, f32[1,1,2048]{2,1,0:T(1,128)S(1)}, f32[1,1,2048,64]{2,3,1,0:T(8,128)S(1)}, s32[32]{0:T(128)S(1)}...) while((s32[]{:T(128)}, f32[1,1,2048]{2,1,0:T(1,128)S(1)}, ...), condition=%wide.region_5.6_spmd.clone, body=%wide.region_1.5_spmd.clone.sunk | while | flops 1141592064 | bytes 120021352 | solution.py:149
  241.2 5.3 %fusion.75 = f32[2048]{0:T(1024)S(1)} fusion(f32[2048,2048]{1,0:T(8,128)S(1)} %get-tuple-element.361, f32[2048]{0:T(1024)S(1)} %bitcast.87, s32[2048]{0:T(1024)S(1)} %get-tuple-element.395, s32[2048]{0:T(1024)S(1)} %fusion.73), kind=kLoop, calls=%fused_computation.4.clone.1 | loop fusion | flops 25163776 | bytes 16809984 | tf_op jit(solution)/shard_map/while/body/eval_jaxpr/reduce_sum | solution.py:89
  246.9 8.2 %fusion.77 = f32[1,1,2048,64]{2,3,1,0:T(8,128)S(1)} fusion(f32[2048,2048]{1,0:T(8,128)} %copy-done, f32[2048]{0:T(1024)S(1)} %bitcast.88, s32[2048]{0:T(1024)S(1)} %get-tuple-element.395, s32[2048]{0:T(1024)S(1)} %fusion.73, bf16[16384,128]{1,0:T(8,128)(2,1)} %get-tuple-element.396, s32[]{:T(128)S(6)} %select_n.248, s32[]{:T(128)S(6)} %add.421, ...), kind=kOutput, calls=%fused_computation.8.clone.1 | convolution fusion | flops 562429952 | bytes 18382856 | tf_op jit(solution)/shard_map/while/body/eval_jaxpr/hgqk,khd->hgqd/dot_general | solution.py:90
  259.4 5.3 %fusion.75 = f32[2048]{0:T(1024)S(1)} fusion(f32[2048,2048]{1,0:T(8,128)S(1)} %get-tuple-element.361, f32[2048]{0:T(1024)S(1)} %bitcast.87, s32[2048]{0:T(1024)S(1)} %get-tuple-element.395, s32[2048]{0:T(1024)S(1)} %fusion.73), kind=kLoop, calls=%fused_computation.4.clone.1 | loop fusion | flops 25163776 | bytes 16809984 | tf_op jit(solution)/shard_map/while/body/eval_jaxpr/reduce_sum | solution.py:89
  265.2 8.2 %fusion.77 = f32[1,1,2048,64]{2,3,1,0:T(8,128)S(1)} fusion(f32[2048,2048]{1,0:T(8,128)} %copy-done, f32[2048]{0:T(1024)S(1)} %bitcast.88, s32[2048]{0:T(1024)S(1)} %get-tuple-element.395, s32[2048]{0:T(1024)S(1)} %fusion.73, bf16[16384,128]{1,0:T(8,128)(2,1)} %get-tuple-element.396, s32[]{:T(128)S(6)} %select_n.248, s32[]{:T(128)S(6)} %add.421, ...), kind=kOutput, calls=%fused_computation.8.clone.1 | convolution fusion | flops 562429952 | bytes 18382856 | tf_op jit(solution)/shard_map/while/body/eval_jaxpr/hgqk,khd->hgqd/dot_general | solution.py:90
  277.7 5.3 %fusion.75 = f32[2048]{0:T(1024)S(1)} fusion(f32[2048,2048]{1,0:T(8,128)S(1)} %get-tuple-element.361, f32[2048]{0:T(1024)S(1)} %bitcast.87, s32[2048]{0:T(1024)S(1)} %get-tuple-element.395, s32[2048]{0:T(1024)S(1)} %fusion.73), kind=kLoop, calls=%fused_computation.4.clone.1 | loop fusion | flops 25163776 | bytes 16809984 | tf_op jit(solution)/shard_map/while/body/eval_jaxpr/reduce_sum | solution.py:89
  283.4 8.2 %fusion.77 = f32[1,1,2048,64]{2,3,1,0:T(8,128)S(1)} fusion(f32[2048,2048]{1,0:T(8,128)} %copy-done, f32[2048]{0:T(1024)S(1)} %bitcast.88, s32[2048]{0:T(1024)S(1)} %get-tuple-element.395, s32[2048]{0:T(1024)S(1)} %fusion.73, bf16[16384,128]{1,0:T(8,128)(2,1)} %get-tuple-element.396, s32[]{:T(128)S(6)} %select_n.248, s32[]{:T(128)S(6)} %add.421, ...), kind=kOutput, calls=%fused_computation.8.clone.1 | convolution fusion | flops 562429952 | bytes 18382856 | tf_op jit(solution)/shard_map/while/body/eval_jaxpr/hgqk,khd->hgqd/dot_general | solution.py:90
  296.0 5.3 %fusion.75 = f32[2048]{0:T(1024)S(1)} fusion(f32[2048,2048]{1,0:T(8,128)S(1)} %get-tuple-element.361, f32[2048]{0:T(1024)S(1)} %bitcast.87, s32[2048]{0:T(1024)S(1)} %get-tuple-element.395, s32[2048]{0:T(1024)S(1)} %fusion.73), kind=kLoop, calls=%fused_computation.4.clone.1 | loop fusion | flops 25163776 | bytes 16809984 | tf_op jit(solution)/shard_map/while/body/eval_jaxpr/reduce_sum | solution.py:89
  301.7 8.2 %fusion.77 = f32[1,1,2048,64]{2,3,1,0:T(8,128)S(1)} fusion(f32[2048,2048]{1,0:T(8,128)} %copy-done, f32[2048]{0:T(1024)S(1)} %bitcast.88, s32[2048]{0:T(1024)S(1)} %get-tuple-element.395, s32[2048]{0:T(1024)S(1)} %fusion.73, bf16[16384,128]{1,0:T(8,128)(2,1)} %get-tuple-element.396, s32[]{:T(128)S(6)} %select_n.248, s32[]{:T(128)S(6)} %add.421, ...), kind=kOutput, calls=%fused_computation.8.clone.1 | convolution fusion | flops 562429952 | bytes 18382856 | tf_op jit(solution)/shard_map/while/body/eval_jaxpr/hgqk,khd->hgqd/dot_general | solution.py:90
  314.2 5.3 %fusion.75 = f32[2048]{0:T(1024)S(1)} fusion(f32[2048,2048]{1,0:T(8,128)S(1)} %get-tuple-element.361, f32[2048]{0:T(1024)S(1)} %bitcast.87, s32[2048]{0:T(1024)S(1)} %get-tuple-element.395, s32[2048]{0:T(1024)S(1)} %fusion.73), kind=kLoop, calls=%fused_computation.4.clone.1 | loop fusion | flops 25163776 | bytes 16809984 | tf_op jit(solution)/shard_map/while/body/eval_jaxpr/reduce_sum | solution.py:89
  319.9 8.2 %fusion.77 = f32[1,1,2048,64]{2,3,1,0:T(8,128)S(1)} fusion(f32[2048,2048]{1,0:T(8,128)} %copy-done, f32[2048]{0:T(1024)S(1)} %bitcast.88, s32[2048]{0:T(1024)S(1)} %get-tuple-element.395, s32[2048]{0:T(1024)S(1)} %fusion.73, bf16[16384,128]{1,0:T(8,128)(2,1)} %get-tuple-element.396, s32[]{:T(128)S(6)} %select_n.248, s32[]{:T(128)S(6)} %add.421, ...), kind=kOutput, calls=%fused_computation.8.clone.1 | convolution fusion | flops 562429952 | bytes 18382856 | tf_op jit(solution)/shard_map/while/body/eval_jaxpr/hgqk,khd->hgqd/dot_general | solution.py:90
  332.5 5.3 %fusion.75 = f32[2048]{0:T(1024)S(1)} fusion(f32[2048,2048]{1,0:T(8,128)S(1)} %get-tuple-element.361, f32[2048]{0:T(1024)S(1)} %bitcast.87, s32[2048]{0:T(1024)S(1)} %get-tuple-element.395, s32[2048]{0:T(1024)S(1)} %fusion.73), kind=kLoop, calls=%fused_computation.4.clone.1 | loop fusion | flops 25163776 | bytes 16809984 | tf_op jit(solution)/shard_map/while/body/eval_jaxpr/reduce_sum | solution.py:89
  338.2 8.2 %fusion.77 = f32[1,1,2048,64]{2,3,1,0:T(8,128)S(1)} fusion(f32[2048,2048]{1,0:T(8,128)} %copy-done, f32[2048]{0:T(1024)S(1)} %bitcast.88, s32[2048]{0:T(1024)S(1)} %get-tuple-element.395, s32[2048]{0:T(1024)S(1)} %fusion.73, bf16[16384,128]{1,0:T(8,128)(2,1)} %get-tuple-element.396, s32[]{:T(128)S(6)} %select_n.248, s32[]{:T(128)S(6)} %add.421, ...), kind=kOutput, calls=%fused_computation.8.clone.1 | convolution fusion | flops 562429952 | bytes 18382856 | tf_op jit(solution)/shard_map/while/body/eval_jaxpr/hgqk,khd->hgqd/dot_general | solution.py:90
  350.7 5.3 %fusion.75 = f32[2048]{0:T(1024)S(1)} fusion(f32[2048,2048]{1,0:T(8,128)S(1)} %get-tuple-element.361, f32[2048]{0:T(1024)S(1)} %bitcast.87, s32[2048]{0:T(1024)S(1)} %get-tuple-element.395, s32[2048]{0:T(1024)S(1)} %fusion.73), kind=kLoop, calls=%fused_computation.4.clone.1 | loop fusion | flops 25163776 | bytes 16809984 | tf_op jit(solution)/shard_map/while/body/eval_jaxpr/reduce_sum | solution.py:89
  356.4 8.2 %fusion.77 = f32[1,1,2048,64]{2,3,1,0:T(8,128)S(1)} fusion(f32[2048,2048]{1,0:T(8,128)} %copy-done, f32[2048]{0:T(1024)S(1)} %bitcast.88, s32[2048]{0:T(1024)S(1)} %get-tuple-element.395, s32[2048]{0:T(1024)S(1)} %fusion.73, bf16[16384,128]{1,0:T(8,128)(2,1)} %get-tuple-element.396, s32[]{:T(128)S(6)} %select_n.248, s32[]{:T(128)S(6)} %add.421, ...), kind=kOutput, calls=%fused_computation.8.clone.1 | convolution fusion | flops 562429952 | bytes 18382856 | tf_op jit(solution)/shard_map/while/body/eval_jaxpr/hgqk,khd->hgqd/dot_general | solution.py:90
  369.0 5.3 %fusion.75 = f32[2048]{0:T(1024)S(1)} fusion(f32[2048,2048]{1,0:T(8,128)S(1)} %get-tuple-element.361, f32[2048]{0:T(1024)S(1)} %bitcast.87, s32[2048]{0:T(1024)S(1)} %get-tuple-element.395, s32[2048]{0:T(1024)S(1)} %fusion.73), kind=kLoop, calls=%fused_computation.4.clone.1 | loop fusion | flops 25163776 | bytes 16809984 | tf_op jit(solution)/shard_map/while/body/eval_jaxpr/reduce_sum | solution.py:89
  374.7 8.2 %fusion.77 = f32[1,1,2048,64]{2,3,1,0:T(8,128)S(1)} fusion(f32[2048,2048]{1,0:T(8,128)} %copy-done, f32[2048]{0:T(1024)S(1)} %bitcast.88, s32[2048]{0:T(1024)S(1)} %get-tuple-element.395, s32[2048]{0:T(1024)S(1)} %fusion.73, bf16[16384,128]{1,0:T(8,128)(2,1)} %get-tuple-element.396, s32[]{:T(128)S(6)} %select_n.248, s32[]{:T(128)S(6)} %add.421, ...), kind=kOutput, calls=%fused_computation.8.clone.1 | convolution fusion | flops 562429952 | bytes 18382856 | tf_op jit(solution)/shard_map/while/body/eval_jaxpr/hgqk,khd->hgqd/dot_general | solution.py:90
  385.2 13.6 %all_to_all.21 = bf16[32,2,2048]{2,1,0:T(2,128)(2,1)S(1)} all-to-all(bf16[32,2,2048]{2,1,0:T(2,128)(2,1)S(1)} %reshape.446), channel_id=1, replica_groups=mesh['grp'=8,'sp'=32] {'sp'}, dimensions={0} | all-to-all | bytes 524288 | tf_op jit(solution)/shard_map/all_to_all | solution.py:152
  (115 shorter events, 53.5 us)
Async XLA Ops:
  6.5 5.1 %copy-start.1 = (s32[32]{0:T(128)S(1)}, s32[32]{0:T(128)}, u32[]{:S(2)}) copy-start(s32[32]{0:T(128)} %param.10) | copy-start | bytes 388
  6.5 61.1 %copy-start.2 = (bf16[2880,64]{0,1:T(8,128)(2,1)S(1)}, bf16[2880,64]{0,1:T(8,128)(2,1)}, u32[]{:S(2)}) copy-start(bf16[2880,64]{0,1:T(8,128)(2,1)} %param.8) | copy-start | bytes 1105924
  6.5 61.1 %all-gather.5.cloned.1.call-start = ((), (), s32[]{:S(2)}) async-start(), calls=%async_computation.2 | async-start | bytes 6217728 | tf_op jit(solution)/shard_map/all_gather | solution.py:32
  8.4 114.2 %all-gather.7.cloned.1.call-start = ((), (), s32[]{:S(2)}) async-start(), calls=%async_computation.3 | async-start | bytes 6217728 | tf_op jit(solution)/shard_map/all_gather | solution.py:32
  130.2 9.2 %copy-start.3 = (f32[32]{0:T(128)S(1)}, f32[32]{0:T(128)}, u32[]{:S(2)}) copy-start(f32[32]{0:T(128)} %param.11) | copy-start | bytes 388
  132.7 103.6 %all-to-all-start = ((bf16[8,2048,128]{2,1,0:T(8,128)(2,1)}), bf16[8,2048,128]{2,1,0:T(8,128)(2,1)}, u32[]{:S(2)}, u32[]{:S(2)}) async-start(bf16[8,2048,128]{2,1,0:T(8,128)(2,1)} %stack.2), calls=%async_computation | async-start | bytes 8388608 | tf_op jit(solution)/shard_map/all_to_all | solution.py:15
  241.2 5.7 %copy-start = (f32[2048,2048]{1,0:T(8,128)}, f32[2048,2048]{1,0:T(8,128)S(1)}, u32[]{:S(2)}) copy-start(f32[2048,2048]{1,0:T(8,128)S(1)} %get-tuple-element.361) | copy-start | bytes 50331652 | tf_op jit(solution)/shard_map/while
  259.4 5.7 %copy-start = (f32[2048,2048]{1,0:T(8,128)}, f32[2048,2048]{1,0:T(8,128)S(1)}, u32[]{:S(2)}) copy-start(f32[2048,2048]{1,0:T(8,128)S(1)} %get-tuple-element.361) | copy-start | bytes 50331652 | tf_op jit(solution)/shard_map/while
  277.7 5.7 %copy-start = (f32[2048,2048]{1,0:T(8,128)}, f32[2048,2048]{1,0:T(8,128)S(1)}, u32[]{:S(2)}) copy-start(f32[2048,2048]{1,0:T(8,128)S(1)} %get-tuple-element.361) | copy-start | bytes 50331652 | tf_op jit(solution)/shard_map/while
  295.9 5.7 %copy-start = (f32[2048,2048]{1,0:T(8,128)}, f32[2048,2048]{1,0:T(8,128)S(1)}, u32[]{:S(2)}) copy-start(f32[2048,2048]{1,0:T(8,128)S(1)} %get-tuple-element.361) | copy-start | bytes 50331652 | tf_op jit(solution)/shard_map/while
  314.2 5.7 %copy-start = (f32[2048,2048]{1,0:T(8,128)}, f32[2048,2048]{1,0:T(8,128)S(1)}, u32[]{:S(2)}) copy-start(f32[2048,2048]{1,0:T(8,128)S(1)} %get-tuple-element.361) | copy-start | bytes 50331652 | tf_op jit(solution)/shard_map/while
  332.4 5.7 %copy-start = (f32[2048,2048]{1,0:T(8,128)}, f32[2048,2048]{1,0:T(8,128)S(1)}, u32[]{:S(2)}) copy-start(f32[2048,2048]{1,0:T(8,128)S(1)} %get-tuple-element.361) | copy-start | bytes 50331652 | tf_op jit(solution)/shard_map/while
  350.7 5.7 %copy-start = (f32[2048,2048]{1,0:T(8,128)}, f32[2048,2048]{1,0:T(8,128)S(1)}, u32[]{:S(2)}) copy-start(f32[2048,2048]{1,0:T(8,128)S(1)} %get-tuple-element.361) | copy-start | bytes 50331652 | tf_op jit(solution)/shard_map/while
  368.9 5.7 %copy-start = (f32[2048,2048]{1,0:T(8,128)}, f32[2048,2048]{1,0:T(8,128)S(1)}, u32[]{:S(2)}) copy-start(f32[2048,2048]{1,0:T(8,128)S(1)} %get-tuple-element.361) | copy-start | bytes 50331652 | tf_op jit(solution)/shard_map/while
Sparse Core Ops, SparseCore 0:
  9.9 57.7 all-gather.4
  70.2 52.4 all-gather.6
